TPU v7x, 32 devices: a whole 2x2x4 slice. The times are simulated.
32 devices in a mesh: gx: 4 (over y, x), gy: 4 (over z), gz: 2 (over core).
Axes of the slice: x: 2, y: 2, z: 4, core: 2. Of those that a mesh axis runs over, the one named last changes fastest.
Arguments:
- seg_rows: bfloat16 [4096, 128, 128], P(('gx', 'gy', 'gz')), may hold values from -6 to 6
- owner_map: int32 [4096, 1], replicated, may hold values from 0 to 31; in each aligned block of 128 rows (0 to 127, 128 to 255, ...) at most 8 rows name the same one
- ghost_pick: int32 [32, 1], P(('gx', 'gy', 'gz')), may hold values from 0 to 127
- slab_cost: int32 [4, 4, 2, 3, 1024], P('gx', 'gy', 'gz'), may hold values from 1 to 24
Outputs:
- forces: bfloat16 [32, 32, 8, 128, 128], P(('gx', 'gy', 'gz'))
- cut_points: float32 [7], replicated
Inputs may be any that keep to these rules, and one draw needn't show every extreme that they name: `owner_map`: among the 128 blocks of one device (aligned runs of 128 rows) no owner is named more than 8 times; some device names some owner exactly 8 times.
All inputs are finite; a program needn't handle non-finite values.
Results may differ from a plain program's by a relative error of at most 0.0034.
Values may be sent and summed in bfloat16 or wider, within the bound.
A program may use at most 128 MiB of HBM per device.

v0:
```python
import math

import jax
import jax.numpy as jnp
from jax import lax
from jax.sharding import PartitionSpec as P

sharpness = 8.0
force_gain = 2.0
radius_eps = 0.001


def padded_2(cells, sides, width):
    for axis, dim in sides:
        count = lax.axis_size(axis)
        head = lax.slice_in_dim(cells, 0, width, axis=dim)
        tail = lax.slice_in_dim(cells, cells.shape[dim] - width, cells.shape[dim], axis=dim)
        cells = jnp.concatenate(
            [
                lax.ppermute(tail, axis, [(i, (i + 1) % count) for i in range(count)]),
                cells,
                lax.ppermute(head, axis, [((i + 1) % count, i) for i in range(count)]),
            ],
            axis=dim,
        )
    return cells


def bisect_cuts(histogram):
    running = jnp.cumsum(histogram, axis=1, dtype=jnp.int32)
    total_cost = running[:, -1]
    below = (2 * running < total_cost[:, None]).astype(jnp.int32)
    position = jnp.sum(below, axis=1, dtype=jnp.int32)
    before = jnp.sum(histogram * below, axis=1, dtype=jnp.int32)
    bins_index = lax.broadcasted_iota(jnp.int32, histogram.shape, 1)
    at_cut = jnp.sum(
        jnp.where(bins_index == position[:, None], histogram, 0), axis=1, dtype=jnp.int32
    )
    remain = (total_cost - 2 * before).astype(jnp.float32)
    return (
        position.astype(jnp.float32) + remain / (2 * at_cut).astype(jnp.float32)
    ) / histogram.shape[1]


def kernel_weights(left_sq, right_sq, inner):
    spread = left_sq + right_sq - 2.0 * inner
    return jnp.exp(-sharpness * spread / (left_sq + right_sq + radius_eps)).astype(jnp.bfloat16)


def pair_forces(slot_rows, ghost_set, ghost_sq):
    rows_f = slot_rows.astype(jnp.float32)
    own_sq = jnp.sum(rows_f * rows_f, axis=-1)
    own_inner = jnp.einsum("sbw,scw->sbc", slot_rows, slot_rows, preferred_element_type=jnp.float32)
    ghost_inner = jnp.einsum(
        "sbw,mw->sbm", slot_rows, ghost_set, preferred_element_type=jnp.float32
    )
    own_kernel = kernel_weights(own_sq[:, :, None], own_sq[:, None, :], own_inner)
    ghost_kernel = kernel_weights(own_sq[:, :, None], ghost_sq[None, None, :], ghost_inner)
    weight_sum = jnp.sum(own_kernel.astype(jnp.float32), axis=-1) + jnp.sum(
        ghost_kernel.astype(jnp.float32), axis=-1
    )
    pulled = jnp.einsum("sbc,scw->sbw", own_kernel, slot_rows, preferred_element_type=jnp.float32)
    pulled = pulled + jnp.einsum(
        "sbm,mw->sbw", ghost_kernel, ghost_set, preferred_element_type=jnp.float32
    )
    return (force_gain * (pulled - weight_sum[..., None] * rows_f)).astype(jnp.bfloat16)


def per_device(seg_rows, owner_map, ghost_pick, slab_cost):
    count_x = lax.axis_size("gx")
    count_y = lax.axis_size("gy")
    count_z = lax.axis_size("gz")
    device_count = count_x * count_y * count_z
    blocks_here, block_rows, width = seg_rows.shape
    capacity = max(2, (2 * blocks_here + device_count - 1) // device_count)
    own_index = lax.axis_index(("gx", "gy", "gz"))
    index_x = lax.axis_index("gx")
    index_y = lax.axis_index("gy")
    local_cost = slab_cost[0, 0, 0]
    bins_count = local_cost.shape[1]
    half_part = index_x // (count_x // 2)
    quarter = half_part * 2 + index_y // (count_y // 2)
    x_term = local_cost[0][None]
    y_term = jnp.where(
        lax.broadcasted_iota(jnp.int32, (2, bins_count), 0) == half_part, local_cost[1][None], 0
    )
    z_term = jnp.where(
        lax.broadcasted_iota(jnp.int32, (4, bins_count), 0) == quarter, local_cost[2][None], 0
    )
    histogram = lax.psum(jnp.concatenate([x_term, y_term, z_term], axis=0), ("gx", "gy", "gz"))
    extent = jnp.array([count_x, count_y, count_y, count_z, count_z, count_z, count_z], jnp.float32)
    cut_points = bisect_cuts(histogram) * extent
    exported = jnp.take(seg_rows, ghost_pick[0], axis=0)
    padded = padded_2(exported[None, None, None], (("gx", 0), ("gy", 1), ("gz", 2)), 1)
    ghost_set = jnp.concatenate(
        [
            padded[0, 1, 1],
            padded[2, 1, 1],
            padded[1, 0, 1],
            padded[1, 2, 1],
            padded[1, 1, 0],
            padded[1, 1, 2],
        ],
        axis=0,
    ).reshape(-1, width)
    ghost_float = ghost_set.astype(jnp.float32)
    ghost_sq = jnp.sum(ghost_float * ghost_float, axis=-1)
    all_owners = owner_map[:, 0].reshape(device_count, blocks_here)
    own_owners = lax.dynamic_index_in_dim(all_owners, own_index, 0, keepdims=False)
    block_order = lax.broadcasted_iota(jnp.int32, (blocks_here,), 0)
    earlier = block_order[:, None] < block_order[None, :]
    same_owner = own_owners[:, None] == own_owners[None, :]
    slot_rank = jnp.sum((same_owner & earlier).astype(jnp.int32), axis=0, dtype=jnp.int32)
    slot_of = own_owners * capacity + slot_rank
    slot_ids = lax.broadcasted_iota(jnp.int32, (device_count * capacity,), 0)
    matches = slot_of[None, :] == slot_ids[:, None]
    source_block = jnp.sum(jnp.where(matches, block_order[None, :], 0), axis=1, dtype=jnp.int32)
    filled = jnp.any(matches, axis=1)
    outgoing = jnp.where(
        filled[:, None, None], jnp.take(seg_rows, source_block, axis=0), jnp.zeros((), jnp.bfloat16)
    )
    outgoing = outgoing.reshape(device_count, capacity, block_rows, width)
    arrivals = jnp.sum((all_owners == own_index).astype(jnp.int32), axis=1, dtype=jnp.int32)
    valid_slot = lax.broadcasted_iota(jnp.int32, (device_count, capacity), 1) < arrivals[:, None]
    received = lax.all_to_all(outgoing, ("gx", "gy", "gz"), split_axis=0, concat_axis=0, tiled=True)
    flat_slots = received.reshape(-1, block_rows, width)
    slot_total = flat_slots.shape[0]
    group_size = math.gcd(slot_total, 16)
    grouped = flat_slots.reshape(slot_total // group_size, group_size, block_rows, width)
    settled = lax.map(lambda piece: pair_forces(piece, ghost_set, ghost_sq), grouped)
    forces = settled.reshape(received.shape)
    forces = jnp.where(valid_slot[:, :, None, None], forces, jnp.zeros((), jnp.bfloat16))
    return (forces[None], cut_points)


def solution(mesh):
    return jax.shard_map(
        per_device,
        mesh=mesh,
        in_specs=(
            P(("gx", "gy", "gz"), None, None),
            P(),
            P(("gx", "gy", "gz"), None),
            P("gx", "gy", "gz", None, None),
        ),
        out_specs=(P(("gx", "gy", "gz"), None, None, None, None), P()),
        check_vma=False,
    )
```

profile of v0, /device:TPU:25, one launch (start us, length us, event | category | flops | bytes accessed | tf_op | source)
XLA Modules:
  0.0 429.4 jit_solution(12656038109581809656)
XLA Ops:
  2.6 10.9 %gather_fusion = bf16[256,128,128]{2,1,0:T(8,128)(2,1)} fusion(bf16[128,128,128]{2,1,0:T(8,128)(2,1)} %param.7, s32[1024]{0:T(1024)S(1)} %pad_clamp_fusion), kind=kCustom, calls=%fused_computation | custom fusion | bytes 16778240 | tf_op jit(solution)/shard_map/jit(_take)/gather | solution.py:120
  13.4 7.4 %select_select_fusion = bf16[32,8,128,128]{3,2,1,0:T(8,128)(2,1)} fusion(bf16[32,8,128,128]{3,2,1,0:T(8,128)(2,1)} %bitcast.108, pred[32,8]{1,0:T(8,128)(4,1)S(1)} %compare_and_fusion, pred[32,8]{1,0:T(8,128)(4,1)S(1)} %broadcast_in_dim.117), kind=kLoop, calls=%fused_computation.37 | loop fusion | flops 8388608 | bytes 16777728 | tf_op jit(solution)/shard_map/jit(_where)/select_n | solution.py:119
  20.8 6.2 %all-to-all-start = ((bf16[32,8,128,128]{3,2,1,0:T(8,128)(2,1)}), bf16[32,8,128,128]{3,2,1,0:T(8,128)(2,1)}, u32[]{:S(2)}, u32[]{:S(2)}) async-start(bf16[32,8,128,128]{3,2,1,0:T(8,128)(2,1)} %select_select_fusion), calls=%async_computation | async-start | bytes 16777216 | tf_op jit(solution)/shard_map/all_to_all | solution.py:125
  31.0 197.4 %psum.7 = s32[7,1024]{1,0:T(8,128)S(1)} all-reduce(s32[7,1024]{1,0:T(8,128)S(1)} %pad_add_fusion), channel_id=1, replica_groups=mesh['gx'=4,'gy'=4,'gz'=2] {'gx','gy','gz'}, use_global_device_ids=true, to_apply=%region_10.11 | all-reduce | flops 7168 | bytes 57344 | tf_op jit(solution)/shard_map/psum | solution.py:90
  236.0 3.0 collective-permute-done.3
  239.1 2.9 collective-permute-start.4
  243.8 178.1 %while.11 = (s32[]{:T(128)}, bf16[16,16,128,128]{3,2,1,0:T(8,128)(2,1)}, bf16[16,16,128,128]{3,2,1,0:T(8,128)(2,1)}, f32[768]{0:T(1024)S(1)}, bf16[768,128]{1,0:T(8,128)(2,1)S(1)}, /*index=5*/s32[]{:T(128)}) while((s32[]{:T(128)}, bf16[16,16,128,128]{3,2,1,0:T(8,128)(2,1)}, bf16[16,16,128,128]{3,2,1,0:T(8,128)(2,1)}, f32[768]{0:T(1024)S(1)}, ...), condition=%wide.region_9.10_spmd, body=%wide.region_5.9_spmd.sunk | while | flops 958394368 | bytes 13063241 | solution.py:130
  245.2 3.5 convert_reduce_fusion.8
  252.1 2.9 fusion.50
  256.4 3.5 convert_reduce_fusion.8
  263.2 2.9 fusion.50
  267.5 3.5 convert_reduce_fusion.8
  274.3 2.9 fusion.50
  278.6 3.5 convert_reduce_fusion.8
  282.1 2.0 convert_reduce_fusion.7
  285.5 2.9 fusion.50
  289.7 3.5 convert_reduce_fusion.8
  296.6 2.9 fusion.50
  300.9 3.5 convert_reduce_fusion.8
  304.3 2.0 convert_reduce_fusion.7
  307.7 2.9 fusion.50
  312.0 3.5 convert_reduce_fusion.8
  318.9 2.9 fusion.50
  323.1 3.5 convert_reduce_fusion.8
  330.0 2.9 fusion.50
  334.2 3.5 convert_reduce_fusion.8
  341.1 2.9 fusion.50
  345.4 3.5 convert_reduce_fusion.8
  348.8 2.0 convert_reduce_fusion.7
  352.2 2.9 fusion.50
  356.5 3.5 convert_reduce_fusion.8
  363.3 2.9 fusion.50
  367.6 3.5 convert_reduce_fusion.8
  371.1 2.0 convert_reduce_fusion.7
  374.5 2.9 fusion.50
  378.7 3.5 convert_reduce_fusion.8
  382.2 2.0 convert_reduce_fusion.7
  385.6 2.9 fusion.50
  389.9 3.5 convert_reduce_fusion.8
  393.4 2.1 convert_reduce_fusion.7
  396.9 2.9 fusion.50
  401.1 3.5 convert_reduce_fusion.8
  404.6 2.0 convert_reduce_fusion.7
  408.0 2.9 fusion.50
  412.3 3.5 convert_reduce_fusion.8
  415.7 2.0 convert_reduce_fusion.7
  419.1 2.9 fusion.50
  422.0 7.4 %broadcast_select_fusion = bf16[1,32,8,128,128]{4,3,2,1,0:T(8,128)(2,1)} fusion(bf16[1,32,8,128,128]{4,3,2,1,0:T(8,128)(2,1)} %bitcast.23, pred[32,8]{1,0:T(8,128)(4,1)S(1)} %iota_compare_fusion.3), kind=kLoop, calls=%fused_computation.38 | loop fusion | flops 4194304 | bytes 16777472 | tf_op jit(solution)/shard_map/jit(_where)/select_n | solution.py:132
  (113 shorter events, 74.4 us)
Async XLA Ops:
  20.8 10.0 %copy-start.1 = (s32[1,1,1,3,1024]{4,2,3,1,0:T(1,128)S(1)}, s32[1,1,1,3,1024]{4,2,3,1,0:T(1,128)}, u32[]{:S(2)}) copy-start(s32[1,1,1,3,1024]{4,2,3,1,0:T(1,128)} %param.10) | copy-start | bytes 36868
  20.8 210.4 %copy-start = (s32[4096,1]{0,1:T(1,128)S(1)}, s32[4096,1]{0,1:T(1,128)}, u32[]{:S(2)}) copy-start(s32[4096,1]{0,1:T(1,128)} %param.8) | copy-start | bytes 49156
  20.8 211.1 %copy-start.2 = (f32[7]{0:T(128)S(1)}, f32[7]{0:T(128)}, u32[]{:S(2)}) copy-start(f32[7]{0:T(128)} %constant.111.clone) | copy-start | bytes 88
  20.8 223.0 %all-to-all-start = ((bf16[32,8,128,128]{3,2,1,0:T(8,128)(2,1)}), bf16[32,8,128,128]{3,2,1,0:T(8,128)(2,1)}, u32[]{:S(2)}, u32[]{:S(2)}) async-start(bf16[32,8,128,128]{3,2,1,0:T(8,128)(2,1)} %select_select_fusion), calls=%async_computation | async-start | bytes 16777216 | tf_op jit(solution)/shard_map/all_to_all | solution.py:125
  28.5 204.0 %collective-permute-start = (bf16[1,1,1,1,128,128]{5,4,3,2,1,0:T(8,128)(2,1)S(1)}, bf16[1,1,1,1,128,128]{5,4,3,2,1,0:T(8,128)(2,1)S(1)}, u32[]{:S(2)}, u32[]{:S(2)}) collective-permute-start(bf16[1,1,1,1,128,128]{5,4,3,2,1,0:T(8,128)(2,1)S(1)} %fusion.32), channel_id=1, source_target_pairs={{0,8},{8,16},{16,24},{24,0},{1,9},{9,17},{17,25},{25,1},{2,10},{10... | collective-permute-start | bytes 98312 | tf_op jit(solution)/shard_map/ppermute | solution.py:20
  29.7 202.8 %collective-permute-start.1 = (bf16[1,1,1,1,128,128]{5,4,3,2,1,0:T(8,128)(2,1)S(1)}, bf16[1,1,1,1,128,128]{5,4,3,2,1,0:T(8,128)(2,1)S(1)}, u32[]{:S(2)}, u32[]{:S(2)}) collective-permute-start(bf16[1,1,1,1,128,128]{5,4,3,2,1,0:T(8,128)(2,1)S(1)} %fusion.32), channel_id=1, source_target_pairs={{8,0},{16,8},{24,16},{0,24},{9,1},{17,9},{25,17},{1,25},{10,2},{18... | collective-permute-start | bytes 98312 | tf_op jit(solution)/shard_map/ppermute | solution.py:22
  232.5 3.5 collective-permute-start.2
  233.8 5.3 %collective-permute-start.3 = (bf16[3,1,1,1,128,128]{5,4,3,2,1,0:T(8,128)(2,1)S(1)}, bf16[3,1,1,1,128,128]{5,4,3,2,1,0:T(8,128)(2,1)S(1)}, u32[]{:S(2)}, u32[]{:S(2)}) collective-permute-start(bf16[3,1,1,1,128,128]{5,4,3,2,1,0:T(8,128)(2,1)S(1)} %pad_maximum_fusion.1), channel_id=1, source_target_pairs={{2,0},{4,2},{6,4},{0,6},{3,1},{5,3},{7,5},{1,7},{10,8},{12,10},{14... | collective-permute-start | bytes 294920 | tf_op jit(solution)/shard_map/ppermute | solution.py:22
  239.1 4.1 collective-permute-start.4
  242.0 1.6 collective-permute-start.5
where the time goes:
time: 435 us; the launch traced here: 429 us
  blocking collectives  197 us (45%)
  matrix products  155 us (36%)
  other arithmetic  42.7 us (10%)
  starting transfers between devices  13.1 us (3%)
  local copies, waits for them, and re-layouts  12.2 us (3%)
  waiting for transfers between devices  6.54 us (2%)
    psum x1, blocking collectives, per_device(): lax.psum(jnp.concatenate([x_term, y_term, z_term], axis=0), ('gx', 'gy',...  197 us
    dot_general x16, matrix products, pair_forces(): jnp.einsum('sbw,mw->sbm', slot_rows, ghost_set, preferred_element_type=jn...  55.7 us
    dot_general x16, matrix products, pair_forces(): jnp.einsum('sbm,mw->sbw', ghost_kernel, ghost_set, preferred_element_type...  46 us
    dot_general x16, matrix products, pair_forces(): jnp.einsum('sbw,scw->sbc', slot_rows, slot_rows, preferred_element_type=j...  32.2 us
    reduce_sum x16, other arithmetic, pair_forces(): own_sq = jnp.sum(rows_f * rows_f, axis=-1)  22.1 us
    dot_general x16, matrix products, pair_forces(): jnp.einsum('sbc,scw->sbw', own_kernel, slot_rows, preferred_element_type=...  21.6 us
    gather x1, local copies, waits for them, and re-layouts, per_device(): jnp.take(seg_rows, source_block, axis=0)  10.9 us
  transfers between devices with their start and end apart: 7, of which 4 were waited for; matrix products, arithmetic and copies ran while one was open for 1% of the time, Pallas kernels for 0%

commit v1 on v0

v1 whole, which is shorter than its diff:
```python
import functools
import math

import jax
import jax.numpy as jnp
from jax import lax
from jax.experimental import pallas as pl
from jax.experimental.pallas import tpu as pltpu
from jax.sharding import PartitionSpec as P

sharpness = 8.0
force_gain = 2.0
radius_eps = 0.001
AXES = ("gx", "gy", "gz")
MESH = pl.DeviceIdType.MESH
LANES = 128


def bisect_cuts(histogram):
    running = jnp.cumsum(histogram, axis=1, dtype=jnp.int32)
    total_cost = running[:, -1]
    below = (2 * running < total_cost[:, None]).astype(jnp.int32)
    position = jnp.sum(below, axis=1, dtype=jnp.int32)
    before = jnp.sum(histogram * below, axis=1, dtype=jnp.int32)
    bins_index = lax.broadcasted_iota(jnp.int32, histogram.shape, 1)
    at_cut = jnp.sum(
        jnp.where(bins_index == position[:, None], histogram, 0), axis=1, dtype=jnp.int32
    )
    remain = (total_cost - 2 * before).astype(jnp.float32)
    return (
        position.astype(jnp.float32) + remain / (2 * at_cut).astype(jnp.float32)
    ) / histogram.shape[1]


def pack_kernel(capacity, source_ref, rows_ref, out_ref):
    owner = pl.program_id(0)
    for slot in range(capacity):
        out_ref[0, slot] = rows_ref[source_ref[owner * capacity + slot]]


def pack_slots(seg_rows, source_block, device_count, capacity):
    _, block_rows, width = seg_rows.shape
    return pl.pallas_call(
        functools.partial(pack_kernel, capacity),
        out_shape=jax.ShapeDtypeStruct((device_count, capacity, block_rows, width), seg_rows.dtype),
        grid_spec=pltpu.PrefetchScalarGridSpec(
            num_scalar_prefetch=1,
            grid=(device_count,),
            in_specs=[pl.BlockSpec(memory_space=pltpu.VMEM)],
            out_specs=pl.BlockSpec(
                (1, capacity, block_rows, width), lambda owner, source: (owner, 0, 0, 0)
            ),
        ),
        name="pack_slots",
    )(source_block, seg_rows)


def square_parts(inner):
    rows = lax.broadcasted_iota(jnp.int32, inner.shape, 0)
    columns = lax.broadcasted_iota(jnp.int32, inner.shape, 1)
    diagonal = jnp.where(rows == columns, inner, 0.0)
    return jnp.sum(diagonal, axis=1, keepdims=True), jnp.sum(diagonal, axis=0, keepdims=True)


def dot_t(left, right):
    return lax.dot_general(
        left, right, (((1,), (1,)), ((), ())), preferred_element_type=jnp.float32
    )


def pair_weights(left_sq, right_sq, inner):
    scale = sharpness * math.log2(math.e)
    ratio = (2.0 * inner + radius_eps) / (left_sq + (right_sq + radius_eps))
    return jnp.exp2(scale * ratio - scale).astype(jnp.bfloat16)


def relay_kernel(
    sizes, capacity, group,
    gain_ref, outgoing_ref, export_ref, cost_ref,
    forces_ref, hist_ref,
    held, ghosts, ghost_aug, ghost_sq, own_aug, hist_cur, hist_in,
    send_sem, recv_sem, out_sem, own_sem, gsend_sem, grecv_sem, hsend_sem, hrecv_sem,
):
    count_x, count_y, count_z = sizes
    device_count = count_x * count_y * count_z
    block_rows, width = export_ref.shape
    coords = tuple(lax.axis_index(axis) for axis in AXES)
    me = (coords[0] * count_y + coords[1]) * count_z + coords[2]

    def coords_of(flat):
        return (flat // (count_y * count_z), (flat // count_z) % count_y, flat % count_z)

    def shifted(axis, offset):
        place = list(coords)
        place[axis] = (coords[axis] + offset + sizes[axis]) % sizes[axis]
        return tuple(place)

    barrier = pltpu.get_barrier_semaphore()

    @pl.loop(1, device_count)
    def _(k):
        pl.semaphore_signal(
            barrier, inc=1, device_id=coords_of((me + k) % device_count), device_id_type=MESH
        )

    pl.semaphore_wait(barrier, device_count - 1)

    ghost_copies = []
    for axis in range(3):
        for side, offset in ((0, 1), (1, -1)):
            index = 2 * axis + side
            copy = pltpu.make_async_remote_copy(
                src_ref=export_ref,
                dst_ref=ghosts.at[pl.ds(index * block_rows, block_rows)],
                send_sem=gsend_sem.at[index],
                recv_sem=grecv_sem.at[index],
                device_id=shifted(axis, offset),
                device_id_type=MESH,
            )
            copy.start()
            ghost_copies.append(copy)

    stage_axes = (1, 0, 2)
    bases = []
    total = 0
    for axis in stage_axes:
        bases.append(total)
        total += sizes[axis] - 1

    def hist_copies(stage):
        axis = stage_axes[stage]
        return [
            pltpu.make_async_remote_copy(
                src_ref=cost_ref if stage == 0 else hist_cur.at[stage - 1],
                dst_ref=hist_in.at[bases[stage] + offset - 1],
                send_sem=hsend_sem.at[bases[stage] + offset - 1],
                recv_sem=hrecv_sem.at[bases[stage] + offset - 1],
                device_id=shifted(axis, offset),
                device_id_type=MESH,
            )
            for offset in range(1, sizes[axis])
        ]

    def hist_start(stage):
        for copy in hist_copies(stage):
            copy.start()

    def hist_finish(stage):
        summed = cost_ref[...] if stage == 0 else hist_cur[stage - 1]
        for index, copy in enumerate(hist_copies(stage)):
            copy.wait()
            summed = summed + hist_in[bases[stage] + index]
        if stage == 2:
            hist_ref[...] = summed
        else:
            hist_cur[stage] = summed

    hist_start(0)

    def big_copy(k):
        target = (me + k) % device_count
        return pltpu.make_async_remote_copy(
            src_ref=outgoing_ref.at[target],
            dst_ref=held.at[me],
            send_sem=send_sem.at[k],
            recv_sem=recv_sem.at[k],
            device_id=coords_of(target),
            device_id_type=MESH,
        )

    def arrival(k):
        source = (me - k + device_count) % device_count
        return pltpu.make_async_remote_copy(
            src_ref=outgoing_ref.at[source],
            dst_ref=held.at[source],
            send_sem=send_sem.at[k],
            recv_sem=recv_sem.at[k],
            device_id=coords_of(source),
            device_id_type=MESH,
        )

    @pl.loop(1, device_count)
    def _(k):
        big_copy(k).start()

    own_copy = pltpu.make_async_copy(outgoing_ref.at[me], held.at[me], own_sem)
    own_copy.start()

    ghost_aug[:, width:] = jnp.ones((ghost_aug.shape[0], width), jnp.bfloat16)
    own_aug[:, :, width:] = jnp.ones((group, block_rows, width), jnp.bfloat16)
    for copy in ghost_copies:
        copy.wait()
    for index in range(6):
        piece = ghosts[pl.ds(index * block_rows, block_rows), :]
        ghost_aug[pl.ds(index * block_rows, block_rows), pl.ds(0, width)] = piece
        _, row_sq = square_parts(dot_t(piece, piece))
        ghost_sq[:, pl.ds(index * block_rows, block_rows)] = row_sq

    own_copy.wait()

    def out_copy(source):
        return pltpu.make_async_copy(held.at[source], forces_ref.at[source], out_sem.at[source])

    @pl.loop(0, device_count)
    def _(k):
        source = (me - k + device_count) % device_count

        @pl.when(k > 0)
        def _():
            arrival(k).wait_recv()

        @pl.loop(0, capacity // group)
        def _(part):
            for inside in range(group):
                slot = part * group + inside
                rows = held[source, slot]
                own_aug[inside, :, pl.ds(0, width)] = rows
                own_inner = dot_t(rows, rows)
                left_sq, right_sq = square_parts(own_inner)
                own_weight = pair_weights(left_sq, right_sq, own_inner)
                ghost_weight = pair_weights(left_sq, ghost_sq[...], dot_t(rows, ghosts[...]))
                pulled = jnp.dot(
                    own_weight, own_aug[inside], preferred_element_type=jnp.float32
                ) + jnp.dot(ghost_weight, ghost_aug[...], preferred_element_type=jnp.float32)
                gain = gain_ref[source * capacity + slot]
                forces = gain * (
                    pulled[:, :width] - pulled[:, width:] * rows.astype(jnp.float32)
                )
                held[source, slot] = forces.astype(jnp.bfloat16)

        out_copy(source).start()
        for stage in range(3):

            @pl.when(k == (stage * device_count) // 4)
            def _():
                hist_finish(stage)
                if stage < 2:
                    hist_start(stage + 1)

    @pl.loop(1, device_count)
    def _(k):
        big_copy(k).wait_send()

    @pl.loop(0, device_count)
    def _(source):
        out_copy(source).wait()


def per_device(seg_rows, owner_map, ghost_pick, slab_cost):
    sizes = tuple(lax.axis_size(axis) for axis in AXES)
    count_x, count_y, count_z = sizes
    device_count = count_x * count_y * count_z
    blocks_here, block_rows, width = seg_rows.shape
    capacity = max(2, (2 * blocks_here + device_count - 1) // device_count)
    own_index = lax.axis_index(AXES)
    index_x = lax.axis_index("gx")
    index_y = lax.axis_index("gy")
    local_cost = slab_cost[0, 0, 0]
    bins_count = local_cost.shape[1]
    half_part = index_x // (count_x // 2)
    quarter = half_part * 2 + index_y // (count_y // 2)
    x_term = local_cost[0][None]
    y_term = jnp.where(
        lax.broadcasted_iota(jnp.int32, (2, bins_count), 0) == half_part, local_cost[1][None], 0
    )
    z_term = jnp.where(
        lax.broadcasted_iota(jnp.int32, (4, bins_count), 0) == quarter, local_cost[2][None], 0
    )
    terms = jnp.concatenate([x_term, y_term, z_term], axis=0).reshape(-1, LANES)
    exported = jnp.take(seg_rows, ghost_pick[0], axis=0)[0]

    all_owners = owner_map[:, 0].reshape(device_count, blocks_here)
    own_owners = lax.dynamic_index_in_dim(all_owners, own_index, 0, keepdims=False)
    block_order = lax.broadcasted_iota(jnp.int32, (blocks_here,), 0)
    earlier = block_order[:, None] < block_order[None, :]
    same_owner = own_owners[:, None] == own_owners[None, :]
    slot_rank = jnp.sum((same_owner & earlier).astype(jnp.int32), axis=0, dtype=jnp.int32)
    slot_of = own_owners * capacity + slot_rank
    slot_ids = lax.broadcasted_iota(jnp.int32, (device_count * capacity,), 0)
    matches = slot_of[None, :] == slot_ids[:, None]
    source_block = jnp.sum(jnp.where(matches, block_order[None, :], 0), axis=1, dtype=jnp.int32)
    arrivals = jnp.sum((all_owners == own_index).astype(jnp.int32), axis=1, dtype=jnp.int32)
    valid_slot = lax.broadcasted_iota(jnp.int32, (device_count, capacity), 1) < arrivals[:, None]
    gain = jnp.where(valid_slot, force_gain, 0.0).astype(jnp.float32).reshape(-1)

    outgoing = pack_slots(seg_rows, source_block, device_count, capacity)

    group = math.gcd(capacity, 2)
    ghost_rows = 6 * block_rows
    hist_rows = terms.shape[0]
    hist_messages = sum(sizes) - 3
    forces, hist = pl.pallas_call(
        functools.partial(relay_kernel, sizes, capacity, group),
        out_shape=(
            jax.ShapeDtypeStruct((device_count, capacity, block_rows, width), jnp.bfloat16),
            jax.ShapeDtypeStruct((hist_rows, LANES), jnp.int32),
        ),
        in_specs=[
            pl.BlockSpec(memory_space=pltpu.SMEM),
            pl.BlockSpec(memory_space=pl.ANY),
            pl.BlockSpec(memory_space=pltpu.VMEM),
            pl.BlockSpec(memory_space=pltpu.VMEM),
        ],
        out_specs=(
            pl.BlockSpec(memory_space=pl.ANY),
            pl.BlockSpec(memory_space=pltpu.VMEM),
        ),
        scratch_shapes=[
            pltpu.VMEM((device_count, capacity, block_rows, width), jnp.bfloat16),
            pltpu.VMEM((ghost_rows, width), jnp.bfloat16),
            pltpu.VMEM((ghost_rows, 2 * width), jnp.bfloat16),
            pltpu.VMEM((1, ghost_rows), jnp.float32),
            pltpu.VMEM((group, block_rows, 2 * width), jnp.bfloat16),
            pltpu.VMEM((2, hist_rows, LANES), jnp.int32),
            pltpu.VMEM((hist_messages, hist_rows, LANES), jnp.int32),
            pltpu.SemaphoreType.DMA((device_count,)),
            pltpu.SemaphoreType.DMA((device_count,)),
            pltpu.SemaphoreType.DMA((device_count,)),
            pltpu.SemaphoreType.DMA,
            pltpu.SemaphoreType.DMA((6,)),
            pltpu.SemaphoreType.DMA((6,)),
            pltpu.SemaphoreType.DMA((hist_messages,)),
            pltpu.SemaphoreType.DMA((hist_messages,)),
        ],
        compiler_params=pltpu.CompilerParams(collective_id=0, has_side_effects=True),
        name="relay_forces",
    )(gain, outgoing, exported, terms)
    extent = jnp.array([count_x, count_y, count_y, count_z, count_z, count_z, count_z], jnp.float32)
    cut_points = bisect_cuts(hist.reshape(-1, bins_count)) * extent
    return (forces[None], cut_points)


def solution(mesh):
    return jax.shard_map(
        per_device,
        mesh=mesh,
        in_specs=(
            P(AXES, None, None),
            P(),
            P(AXES, None),
            P("gx", "gy", "gz", None, None),
        ),
        out_specs=(P(AXES, None, None, None, None), P()),
        check_vma=False,
    )
```

time: 435 us -> 252 us (0.58); the launches traced: 429 us -> 251 us
  Pallas kernels: 0 us -> 226 us
  blocking collectives: 197 us -> 0 us
  matrix products: 155 us -> 0 us
  other arithmetic: 42.7 us -> 9.32 us
  starting transfers between devices: 13.1 us -> 0 us
  waiting for transfers between devices: 6.54 us -> 0 us
    pallas_call x0 -> x2, Pallas kernels: none -> 226 us  [the longest x1 212 us: per_device(): pl.pallas_call(functools.partial(relay_kernel, sizes, capacity, group), o...]
    psum x1 -> x0, blocking collectives: 197 us -> none  [per_device(): lax.psum(jnp.concatenate([x_term, y_term, z_term], axis=0), ('gx', 'gy',...]
    dot_general x64 -> x0, matrix products: 155 us -> none  [the longest x16 55.7 us: pair_forces(): jnp.einsum('sbw,mw->sbm', slot_rows, ghost_set, preferred_element_type=jn...]
    reduce_sum x17 -> x1, other arithmetic: 22.3 us -> 0.12 us  [bisect_cuts(): jnp.sum(jnp.where(bins_index == position[:, None], histogram, 0), axis=1,...]
    select_n x4 -> x2, other arithmetic: 15.6 us -> 1.44 us  [the longest x1 1.37 us: per_device(): exported = jnp.take(seg_rows, ghost_pick[0], axis=0)[0]]
    gather x1 -> x0, local copies, waits for them, and re-layouts: 10.9 us -> none  [per_device(): jnp.take(seg_rows, source_block, axis=0)]
    unnamed x14 -> x5, local copies, waits for them, and re-layouts: 0.17 us -> 10.5 us
    ppermute x6 -> x0, starting transfers between devices: 6.89 us -> none  [the longest x3 5.4 us: padded_2(): lax.ppermute(tail, axis, [(i, (i + 1) % count) for i in range(count)])]
  transfers between devices with their start and end apart: 7 -> 0, of which waited for: 4 -> 0; matrix products, arithmetic and copies ran while one was open for 1% -> 0% of each run, Pallas kernels for 0% -> 0%
where the time goes in v1:
time: 252 us; the launch traced here: 251 us
  Pallas kernels  226 us (90%)
  local copies, waits for them, and re-layouts  14.3 us (6%)
  other arithmetic  9.32 us (4%)
    pallas_call x1, Pallas kernels, per_device(): pl.pallas_call(functools.partial(relay_kernel, sizes, capacity, group), o...  212 us
    pallas_call x1, Pallas kernels, pack_slots(): pl.pallas_call(functools.partial(pack_kernel, capacity), out_shape=jax.Sh...  14.6 us
    unnamed x5, local copies, waits for them, and re-layouts  10.5 us

profile of v1, /device:TPU:25, one launch (start us, length us, event | category | flops | bytes accessed | tf_op | source)
XLA Modules:
  0.0 251.3 jit_solution(13511019064587859297)
XLA Ops:
  0.6 0.0 copy-start
  0.7 0.7 slice_bitcast_fusion
  1.4 0.1 broadcast_select_fusion
  1.5 0.1 broadcast_select_fusion.1
  1.6 0.6 reshape.64.cost_ref
  2.2 0.7 fusion.6
  2.9 0.1 convert_reduce_fusion
  3.0 0.7 fusion.5
  3.7 0.7 select_reduce_fusion.source_ref
  4.4 0.0 copy-start.1
  4.4 14.6 %pack_slots.1.outgoing_ref = bf16[32,8,128,128]{3,2,1,0:T(8,128)(2,1)} custom-call(s32[256]{0:T(256)} %select_reduce_fusion.source_ref, bf16[128,128,128]{2,1,0:T(8,128)(2,1)} %rows_ref.1), custom_call_target="tpu_custom_call" | custom-call | tf_op jit(solution)/shard_map/pack_slots/pallas_call | solution.py:43
  19.7 1.4 fusion.1.export_ref
  21.0 0.0 copy-done
  21.0 0.1 convert_reduce_fusion.2
  21.2 0.1 fusion.4
  21.2 0.7 select_n.53.gain_ref
  21.9 211.6 %relay_forces.1 = (bf16[32,8,128,128]{3,2,1,0:T(8,128)(2,1)}, s32[56,128]{1,0:T(8,128)}) custom-call(f32[256]{0:T(256)} %select_n.53.gain_ref, bf16[32,8,128,128]{3,2,1,0:T(8,128)(2,1)} %pack_slots.1.outgoing_ref, bf16[128,128]{1,0:T(8,128)(2,1)} %fusion.1.export_ref, s32[56,128]{1,0:T(8,128)} %reshape.64.cost_ref), custom_call_target="tpu_custom_call" | custom-call | tf_op jit(solution)/shard_map/relay_forces/pallas_call | solution.py:292
  233.5 3.8 %reduce-window.6 = s32[7,8,128]{2,1,0:T(8,128)S(1)} reduce-window(s32[7,8,128]{2,1,0:T(8,128)} %bitcast.44, s32[]{:T(128)} %constant.63.clone.1), window={size=1x1x128 pad=0_0x0_0x127_0}, to_apply=%region_3.4 | reduce-window | flops 910336 | bytes 57348 | tf_op jit(solution)/shard_map/reduce-window
  237.4 0.3 slice_reduce_fusion
  237.7 0.2 reduce-window.9
  237.8 0.1 broadcast_add_fusion
  237.9 0.2 copy.10
  238.1 0.3 convert_reduce_fusion.1
  238.4 0.1 eq.81
  238.5 0.1 eq.82
  238.6 0.1 lt.61
  238.7 0.1 lt.62
  238.8 0.1 reshape.68
  238.8 0.9 select_reduce_fusion.2
  239.8 0.1 reduce_sum.76
  239.9 0.1 reduce_sum.77
  240.0 0.1 reduce_sum.79
  240.1 0.1 reduce_sum.80
  240.2 0.0 copy-done.1
  240.2 0.5 multiply_multiply_fusion
  240.7 10.5 %copy.13 = bf16[1,32,8,128,128]{4,3,2,1,0:T(8,128)(2,1)} copy(bf16[1,32,8,128,128]{4,3,2,1,0:T(8,128)(2,1)} %bitcast.41) | data formatting | bytes 16777216
  (5 shorter events, 0.0 us)
Async XLA Ops:
  0.6 20.4 %copy-start = (s32[4096,1]{0,1:T(1,128)S(1)}, s32[4096,1]{0,1:T(1,128)}, u32[]{:S(2)}) copy-start(s32[4096,1]{0,1:T(1,128)} %param.6) | copy-start | bytes 49156
  4.4 235.8 %copy-start.1 = (f32[7]{0:T(128)S(1)}, f32[7]{0:T(128)}, u32[]{:S(2)}) copy-start(f32[7]{0:T(128)} %constant.76.clone) | copy-start | bytes 88

commit v2 on v1

v2 whole, which is shorter than its diff:
```python
import functools
import math

import jax
import jax.numpy as jnp
from jax import lax
from jax.experimental import pallas as pl
from jax.experimental.pallas import tpu as pltpu
from jax.sharding import PartitionSpec as P

sharpness = 8.0
force_gain = 2.0
radius_eps = 0.001
AXES = ("gx", "gy", "gz")
MESH = pl.DeviceIdType.MESH
LANES = 128
SHARES = (2, 3, 4, 8)


def bisect_cuts(histogram):
    running = jnp.cumsum(histogram, axis=1, dtype=jnp.int32)
    total_cost = running[:, -1]
    below = (2 * running < total_cost[:, None]).astype(jnp.int32)
    position = jnp.sum(below, axis=1, dtype=jnp.int32)
    before = jnp.sum(histogram * below, axis=1, dtype=jnp.int32)
    bins_index = lax.broadcasted_iota(jnp.int32, histogram.shape, 1)
    at_cut = jnp.sum(
        jnp.where(bins_index == position[:, None], histogram, 0), axis=1, dtype=jnp.int32
    )
    remain = (total_cost - 2 * before).astype(jnp.float32)
    return (
        position.astype(jnp.float32) + remain / (2 * at_cut).astype(jnp.float32)
    ) / histogram.shape[1]


def square_parts(inner):
    rows = lax.broadcasted_iota(jnp.int32, inner.shape, 0)
    columns = lax.broadcasted_iota(jnp.int32, inner.shape, 1)
    diagonal = jnp.where(rows == columns, inner, 0.0)
    return jnp.sum(diagonal, axis=1, keepdims=True), jnp.sum(diagonal, axis=0, keepdims=True)


def dot_t(left, right):
    return lax.dot_general(
        left, right, (((1,), (1,)), ((), ())), preferred_element_type=jnp.float32
    )


def pair_weights(left_sq, right_sq, inner):
    scale = sharpness * math.log2(math.e)
    ratio = (2.0 * inner + radius_eps) / (left_sq + (right_sq + radius_eps))
    return jnp.exp2(scale * ratio - scale).astype(jnp.bfloat16)


def relay_kernel(
    sizes, capacity, halves, group, limit,
    pack_ref, forward_ref, gain_ref, rows_ref, export_ref, cost_ref,
    forces_ref, hist_ref,
    held, stage_out, ghosts, ghost_aug, ghost_sq, own_aug, hist_cur, hist_in,
    send_sem, recv_sem, out_sem, zsend_sem, zrecv_sem,
    gsend_sem, grecv_sem, hsend_sem, hrecv_sem, *z_refs,
):
    count_x, count_y, count_z = sizes
    device_count = count_x * count_y * count_z
    plane = count_x * count_z
    part = capacity // halves
    plane_slots = plane * capacity
    first = plane * part
    block_rows, width = export_ref.shape
    coords = tuple(lax.axis_index(axis) for axis in AXES)
    me = (coords[0] * count_y + coords[1]) * count_z + coords[2]
    my_spot = coords[0] * count_z + coords[2]
    steps = halves * count_y
    bounds = [(0, first), (first, limit)][:halves]
    pieces = [(half, offset) for half in range(halves) for offset in range(1, count_y)]
    z_out = dict(zip(pieces, z_refs[: len(pieces)]))
    z_in = dict(zip(pieces, z_refs[len(pieces) :]))

    def coords_of(flat):
        return (flat // (count_y * count_z), (flat // count_z) % count_y, flat % count_z)

    def shifted(axis, offset):
        place = list(coords)
        place[axis] = (coords[axis] + offset + sizes[axis]) % sizes[axis]
        return tuple(place)

    barrier = pltpu.get_barrier_semaphore()

    @pl.loop(1, device_count)
    def _(k):
        pl.semaphore_signal(
            barrier, inc=1, device_id=coords_of((me + k) % device_count), device_id_type=MESH
        )

    def z_pack(half, offset):
        low, high = bounds[half]

        @pl.loop(0, high - low)
        def _(place):
            z_out[half, offset][place] = rows_ref[pack_ref[offset * plane_slots + low + place]]

    def z_copy(half, offset):
        index = pieces.index((half, offset))
        return pltpu.make_async_remote_copy(
            src_ref=z_out[half, offset],
            dst_ref=z_in[half, offset],
            send_sem=zsend_sem.at[index],
            recv_sem=zrecv_sem.at[index],
            device_id=shifted(1, offset),
            device_id_type=MESH,
        )

    z_pack(*pieces[0])
    pl.semaphore_wait(barrier, device_count - 1)

    ghost_copies = []
    for axis in range(3):
        for side, offset in ((0, 1), (1, -1)):
            index = 2 * axis + side
            copy = pltpu.make_async_remote_copy(
                src_ref=export_ref,
                dst_ref=ghosts.at[pl.ds(index * block_rows, block_rows)],
                send_sem=gsend_sem.at[index],
                recv_sem=grecv_sem.at[index],
                device_id=shifted(axis, offset),
                device_id_type=MESH,
            )
            copy.start()
            ghost_copies.append(copy)

    stage_axes = (1, 0, 2)
    bases = []
    total = 0
    for axis in stage_axes:
        bases.append(total)
        total += sizes[axis] - 1

    def hist_copies(stage):
        axis = stage_axes[stage]
        return [
            pltpu.make_async_remote_copy(
                src_ref=cost_ref if stage == 0 else hist_cur.at[stage - 1],
                dst_ref=hist_in.at[bases[stage] + offset - 1],
                send_sem=hsend_sem.at[bases[stage] + offset - 1],
                recv_sem=hrecv_sem.at[bases[stage] + offset - 1],
                device_id=shifted(axis, offset),
                device_id_type=MESH,
            )
            for offset in range(1, sizes[axis])
        ]

    def hist_start(stage):
        for copy in hist_copies(stage):
            copy.start()

    def hist_finish(stage):
        summed = cost_ref[...] if stage == 0 else hist_cur[stage - 1]
        for index, copy in enumerate(hist_copies(stage)):
            copy.wait()
            summed = summed + hist_in[bases[stage] + index]
        if stage == 2:
            hist_ref[...] = summed
        else:
            hist_cur[stage] = summed

    hist_start(0)
    for index, piece in enumerate(pieces):
        if index + 1 < len(pieces):
            z_pack(*pieces[index + 1])
        z_copy(*piece).start()

    def spot_shift(away):
        return (my_spot + away + plane) % plane

    def device_at(spot):
        return (spot // count_z, coords[1], spot % count_z)

    def source_at(spot, offset):
        row = (coords[1] - offset + count_y) % count_y
        return ((spot // count_z) * count_y + row) * count_z + spot % count_z

    def step_parts(step):
        return step // count_y, step % count_y

    def forward_copy(step, away):
        half, offset = step_parts(step)
        spot = spot_shift(away)
        return pltpu.make_async_remote_copy(
            src_ref=stage_out.at[step, away],
            dst_ref=held.at[source_at(my_spot, offset), pl.ds(half * part, part)],
            send_sem=send_sem.at[step * plane + away],
            recv_sem=recv_sem.at[step * plane + away],
            device_id=device_at(spot),
            device_id_type=MESH,
        )

    def arrival(step, away):
        half, offset = step_parts(step)
        spot = spot_shift(-away)
        return pltpu.make_async_remote_copy(
            src_ref=stage_out.at[step, away],
            dst_ref=held.at[source_at(spot, offset), pl.ds(half * part, part)],
            send_sem=send_sem.at[step * plane + away],
            recv_sem=recv_sem.at[step * plane + away],
            device_id=device_at(spot),
            device_id_type=MESH,
        )

    def slot_value(half, offset, spot, inside):
        index = spot * capacity + half * part + inside
        if offset == 0:
            return rows_ref[pack_ref[index]]
        place = forward_ref[offset * plane_slots + index]
        if half == 0:
            return z_in[0, offset][place]
        early = z_in[0, offset][jnp.minimum(place, first - 1)]
        late = z_in[1, offset][jnp.clip(place - first, 0, limit - first - 1)]
        is_early = jnp.full(early.shape, place, jnp.int32) < first
        return jnp.where(is_early, early, late)

    def forward(half, offset):
        step = half * count_y + offset
        if offset > 0:
            z_copy(half, offset).wait_recv()

        @pl.loop(1, plane)
        def _(away):
            for inside in range(part):
                stage_out[step, away, inside] = slot_value(half, offset, spot_shift(away), inside)

            @pl.when(away > 1)
            def _():
                forward_copy(step, away - 1).start()

        own = source_at(my_spot, offset)
        for inside in range(part):
            held[own, half * part + inside] = slot_value(half, offset, my_spot, inside)
        forward_copy(step, plane - 1).start()

    def out_copy(step, away):
        half, offset = step_parts(step)
        source = source_at(spot_shift(-away), offset)
        return pltpu.make_async_copy(
            held.at[source, pl.ds(half * part, part)],
            forces_ref.at[source, pl.ds(half * part, part)],
            out_sem.at[step * plane + away],
        )

    def compute(step):
        half, offset = step_parts(step)

        @pl.loop(0, plane)
        def _(away):
            source = source_at(spot_shift(-away), offset)

            @pl.when(away > 0)
            def _():
                arrival(step, away).wait_recv()

            @pl.loop(0, part // group)
            def _(pair):
                for inside in range(group):
                    slot = half * part + pair * group + inside
                    rows = held[source, slot]
                    own_aug[inside, :, pl.ds(0, width)] = rows
                    own_inner = dot_t(rows, rows)
                    left_sq, right_sq = square_parts(own_inner)
                    own_weight = pair_weights(left_sq, right_sq, own_inner)
                    ghost_weight = pair_weights(left_sq, ghost_sq[...], dot_t(rows, ghosts[...]))
                    pulled = jnp.dot(
                        own_weight, own_aug[inside], preferred_element_type=jnp.float32
                    ) + jnp.dot(ghost_weight, ghost_aug[...], preferred_element_type=jnp.float32)
                    gain = gain_ref[source * capacity + slot]
                    forces = gain * (
                        pulled[:, :width] - pulled[:, width:] * rows.astype(jnp.float32)
                    )
                    held[source, slot] = forces.astype(jnp.bfloat16)

            out_copy(step, away).start()

    @pl.loop(0, steps + 1)
    def _(step):
        for half in range(halves):
            for offset in range(count_y):

                @pl.when(step == half * count_y + offset)
                def _():
                    forward(half, offset)

        @pl.when(step == 0)
        def _():
            ghost_aug[:, width:] = jnp.ones((ghost_aug.shape[0], width), jnp.bfloat16)
            own_aug[:, :, width:] = jnp.ones((group, block_rows, width), jnp.bfloat16)
            for copy in ghost_copies:
                copy.wait()
            for index in range(6):
                piece = ghosts[pl.ds(index * block_rows, block_rows), :]
                ghost_aug[pl.ds(index * block_rows, block_rows), pl.ds(0, width)] = piece
                _, row_sq = square_parts(dot_t(piece, piece))
                ghost_sq[:, pl.ds(index * block_rows, block_rows)] = row_sq

        for stage in range(3):

            @pl.when(step == 1 + (stage * steps) // 4)
            def _():
                hist_finish(stage)
                if stage < 2:
                    hist_start(stage + 1)

        @pl.when(step > 0)
        def _():
            compute(step - 1)

    for piece in pieces:
        z_copy(*piece).wait_send()

    @pl.loop(0, steps)
    def _(step):
        @pl.loop(0, plane)
        def _(away):
            @pl.when(away > 0)
            def _():
                forward_copy(step, away).wait_send()

            out_copy(step, away).wait()


def per_device(seg_rows, owner_map, ghost_pick, slab_cost):
    sizes = tuple(lax.axis_size(axis) for axis in AXES)
    count_x, count_y, count_z = sizes
    device_count = count_x * count_y * count_z
    blocks_here, block_rows, width = seg_rows.shape
    capacity = max(2, (2 * blocks_here + device_count - 1) // device_count)
    own_index = lax.axis_index(AXES)
    index_x = lax.axis_index("gx")
    index_y = lax.axis_index("gy")
    local_cost = slab_cost[0, 0, 0]
    bins_count = local_cost.shape[1]
    half_part = index_x // (count_x // 2)
    quarter = half_part * 2 + index_y // (count_y // 2)
    x_term = local_cost[0][None]
    y_term = jnp.where(
        lax.broadcasted_iota(jnp.int32, (2, bins_count), 0) == half_part, local_cost[1][None], 0
    )
    z_term = jnp.where(
        lax.broadcasted_iota(jnp.int32, (4, bins_count), 0) == quarter, local_cost[2][None], 0
    )
    terms = jnp.concatenate([x_term, y_term, z_term], axis=0).reshape(-1, LANES)
    exported = jnp.take(seg_rows, ghost_pick[0], axis=0)[0]

    all_owners = owner_map[:, 0].reshape(device_count, blocks_here)
    own_owners = lax.dynamic_index_in_dim(all_owners, own_index, 0, keepdims=False)
    block_order = lax.broadcasted_iota(jnp.int32, (blocks_here,), 0)
    earlier = block_order[:, None] < block_order[None, :]
    same_owner = own_owners[:, None] == own_owners[None, :]
    slot_rank = jnp.sum((same_owner & earlier).astype(jnp.int32), axis=0, dtype=jnp.int32)
    index_z = lax.axis_index("gz")
    plane = count_x * count_z
    plane_slots = plane * capacity

    def row_of(owner):
        return (owner // count_z) % count_y

    def spot_of(owner):
        return owner // (count_y * count_z) * count_z + owner % count_z

    own_offset = (row_of(own_owners) - index_y + count_y) % count_y
    own_spot = spot_of(own_owners)
    order = slot_rank * plane + own_spot
    ahead = (own_offset[:, None] == own_offset[None, :]) & (order[:, None] < order[None, :])
    compact = jnp.sum(ahead.astype(jnp.int32), axis=0, dtype=jnp.int32)
    place = jnp.where(own_offset == 0, own_spot * capacity + slot_rank, compact)
    place = own_offset * plane_slots + place
    place_ids = lax.broadcasted_iota(jnp.int32, (count_y * plane_slots,), 0)
    matches = place[None, :] == place_ids[:, None]
    pack_index = jnp.sum(jnp.where(matches, block_order[None, :], 0), axis=1, dtype=jnp.int32)

    line = lax.dynamic_index_in_dim(
        all_owners.reshape(count_x, count_y, count_z, blocks_here), index_x, 0, keepdims=False
    )
    line = lax.dynamic_index_in_dim(line, index_z, 1, keepdims=False)
    here = jnp.where(row_of(line) == index_y, spot_of(line), -1)
    spots = lax.broadcasted_iota(jnp.int32, (plane,), 0)
    ranks = lax.broadcasted_iota(jnp.int32, (capacity,), 0)
    named = jnp.sum(
        (here[:, None, :] == spots[None, :, None]).astype(jnp.int32), axis=2, dtype=jnp.int32
    )
    lower = jnp.sum(
        jnp.minimum(named[:, :, None], ranks[None, None, :]), axis=1, dtype=jnp.int32
    )
    beside = jnp.sum(
        (
            (named[:, None, :, None] > ranks[None, None, None, :])
            & (spots[None, None, :, None] < spots[None, :, None, None])
        ).astype(jnp.int32),
        axis=2,
        dtype=jnp.int32,
    )
    by_row = lower[:, None, :] + beside
    by_row = jnp.concatenate([by_row, by_row], axis=0)[::-1]
    forward_index = lax.dynamic_slice_in_dim(
        by_row, count_y - 1 - index_y, count_y, axis=0
    ).reshape(-1)

    all_rows = row_of(all_owners)
    source_rows = row_of(lax.broadcasted_iota(jnp.int32, (device_count, 1), 0))
    crowd = jnp.max(
        jnp.stack(
            [
                jnp.sum(((all_rows == row) & (source_rows != row)).astype(jnp.int32), axis=1)
                for row in range(count_y)
            ]
        )
    )
    arrivals = jnp.sum((all_owners == own_index).astype(jnp.int32), axis=1, dtype=jnp.int32)
    valid_slot = lax.broadcasted_iota(jnp.int32, (device_count, capacity), 1) < arrivals[:, None]
    gain = jnp.where(valid_slot, force_gain, 0.0).astype(jnp.float32).reshape(-1)

    halves = 2 if capacity % 2 == 0 else 1
    part = capacity // halves
    group = math.gcd(part, 2)
    first = plane * part
    rest = plane_slots - first
    limits = sorted({first + max(1, rest * share // 8) for share in SHARES}) if rest else [first]
    ghost_rows = 6 * block_rows
    hist_rows = terms.shape[0]
    hist_messages = sum(sizes) - 3
    steps = halves * count_y

    def relay(collective_id, limit):
        lengths = [first, limit - first][:halves]
        z_shapes = [
            pltpu.VMEM((length, block_rows, width), jnp.bfloat16)
            for length in lengths
            for _ in range(1, count_y)
        ]
        z_count = len(z_shapes)
        return pl.pallas_call(
            functools.partial(relay_kernel, sizes, capacity, halves, group, limit),
            out_shape=(
                jax.ShapeDtypeStruct((device_count, capacity, block_rows, width), jnp.bfloat16),
                jax.ShapeDtypeStruct((hist_rows, LANES), jnp.int32),
            ),
            in_specs=[pl.BlockSpec(memory_space=pltpu.SMEM)] * 3
            + [pl.BlockSpec(memory_space=pltpu.VMEM)] * 3,
            out_specs=(
                pl.BlockSpec(memory_space=pl.ANY),
                pl.BlockSpec(memory_space=pltpu.VMEM),
            ),
            scratch_shapes=[
                pltpu.VMEM((device_count, capacity, block_rows, width), jnp.bfloat16),
                pltpu.VMEM((steps, plane, part, block_rows, width), jnp.bfloat16),
                pltpu.VMEM((ghost_rows, width), jnp.bfloat16),
                pltpu.VMEM((ghost_rows, 2 * width), jnp.bfloat16),
                pltpu.VMEM((1, ghost_rows), jnp.float32),
                pltpu.VMEM((group, block_rows, 2 * width), jnp.bfloat16),
                pltpu.VMEM((2, hist_rows, LANES), jnp.int32),
                pltpu.VMEM((hist_messages, hist_rows, LANES), jnp.int32),
                pltpu.SemaphoreType.DMA((steps * plane,)),
                pltpu.SemaphoreType.DMA((steps * plane,)),
                pltpu.SemaphoreType.DMA((steps * plane,)),
                pltpu.SemaphoreType.DMA((z_count,)),
                pltpu.SemaphoreType.DMA((z_count,)),
                pltpu.SemaphoreType.DMA((6,)),
                pltpu.SemaphoreType.DMA((6,)),
                pltpu.SemaphoreType.DMA((hist_messages,)),
                pltpu.SemaphoreType.DMA((hist_messages,)),
            ]
            + z_shapes * 2,
            compiler_params=pltpu.CompilerParams(
                collective_id=collective_id,
                has_side_effects=True,
                vmem_limit_bytes=60 * 1024 * 1024,
            ),
            name=f"relay_forces_{limit}",
        )

    operands = (pack_index, forward_index, gain, seg_rows, exported, terms)
    if len(limits) > 1:
        choice = sum((crowd > limit).astype(jnp.int32) for limit in limits[:-1])
        forces, hist = lax.switch(
            choice, [relay(index, limit) for index, limit in enumerate(limits)], *operands
        )
    else:
        forces, hist = relay(0, limits[0])(*operands)
    extent = jnp.array([count_x, count_y, count_y, count_z, count_z, count_z, count_z], jnp.float32)
    cut_points = bisect_cuts(hist.reshape(-1, bins_count)) * extent
    return (forces[None], cut_points)


def solution(mesh):
    return jax.shard_map(
        per_device,
        mesh=mesh,
        in_specs=(
            P(AXES, None, None),
            P(),
            P(AXES, None),
            P("gx", "gy", "gz", None, None),
        ),
        out_specs=(P(AXES, None, None, None, None), P()),
        check_vma=False,
    )
```

time: 252 us -> 240 us (0.952)
  Pallas kernels: 226 us -> 208 us
  between operations: 1.4 us -> 4.1 us
    pallas_call x2 -> x1, Pallas kernels: 226 us -> 208 us  [per_device(): lax.switch(choice, [relay(index, limit) for index, limit in enumerate(lim...]
    reduce_max x0 -> x4, other arithmetic: none -> 2.54 us  [per_device(): jnp.max(jnp.stack([jnp.sum(((all_rows == row) & (source_rows != row)).ast...]
    unnamed x5 -> x3, local copies, waits for them, and re-layouts: 10.5 us -> 10.5 us
where the time goes in v2:
time: 240 us; the launch traced here: 239 us
  Pallas kernels  208 us (87%)
  local copies, waits for them, and re-layouts  14.9 us (6%)
  other arithmetic  11.6 us (5%)
  between operations  4.1 us (2%)
    pallas_call x1, Pallas kernels, per_device(): lax.switch(choice, [relay(index, limit) for index, limit in enumerate(lim...  208 us
    unnamed x3, local copies, waits for them, and re-layouts  10.5 us

profile of v2, /device:TPU:25, one launch (start us, length us, event | category | flops | bytes accessed | tf_op | source)
XLA Modules:
  0.0 239.1 jit_solution(5081021137236158626)
XLA Ops:
  0.7 0.7 slice_bitcast_fusion
  1.4 0.1 broadcast_select_fusion
  1.5 0.1 broadcast_select_fusion.1
  1.6 0.7 and_select_fusion.2
  2.3 0.1 convert_reduce_fusion.1
  2.5 0.1 and_convert_fusion
  2.6 0.7 constant_dynamic-slice_fusion.4
  3.3 0.1 convert_reduce_fusion.3
  3.4 0.1 iota_compare_fusion.1
  3.5 0.1 convert_reduce_fusion
  3.6 0.1 minimum_reduce_fusion
  3.8 0.7 compare_convert_fusion
  5.2 0.9 convert_reduce_fusion.4
  6.2 0.6 reduce_max.23
  6.8 0.6 reduce_max.24
  8.8 0.6 reduce_max.29
  10.0 0.6 reduce_max.38
  11.3 0.0 copy-start
  11.4 212.6 %conditional.1 = (s32[56,128]{1,0:T(8,128)S(1)}, bf16[1,32,8,128,128]{4,3,2,1,0:T(8,128)(2,1)}) conditional(s32[]{:T(128)} %clamp.11, (s32[1,128]{1,0:T(1,128)S(1)}, s32[1,128]{1,0:T(1,128)S(1)}, s32[1,128]{1,0:T(1,128)S(1)}, s32[1,128]{1,0:T(1,128)S(1)}, s32[1,128]{1,0:T(1,128)S(1)}, ...), branch_computations={%region_12.16_spmd, %region_16.20_spmd, %region_20.24_spmd, %regio... | conditional | flops 136038 | bytes 481112 | solution.py:481
  11.4 1.4 fusion.3.export_ref
  12.8 0.6 reshape.437.forward_ref
  13.4 0.6 reshape.438.cost_ref
  14.0 0.1 reduce_sum.163
  14.1 0.1 compare_select_fusion.2
  14.2 0.7 select_n.304.gain_ref
  14.9 0.7 select_reduce_fusion.1.pack_ref
  15.5 208.2 %relay_forces_44.2 = (bf16[32,8,128,128]{3,2,1,0:T(8,128)(2,1)}, s32[56,128]{1,0:T(8,128)S(1)}) custom-call(s32[256]{0:T(256)} %select_reduce_fusion.1.pack_ref, s32[256]{0:T(256)} %reshape.437.forward_ref, f32[256]{0:T(256)} %select_n.304.gain_ref, bf16[128,128,128]{2,1,0:T(8,128)(2,1)} %get-tuple-element.679.rows_ref, bf16[128,128]{1,0:T(8,128)(2,1)} %fusion.3.export_ref, ...), custom_call_target="tpu_custom_call" | custom-call | tf_op jit(solution)/shard_map/cond/branch_1_fun/relay_forces_44/pallas_call | solution.py:481
  224.0 2.0 reduce-window.6
  226.0 0.3 slice_reduce_fusion
  226.2 0.2 reduce-window.9
  226.4 0.1 broadcast_add_fusion
  226.5 0.2 copy.10
  226.7 0.3 convert_reduce_fusion.2
  227.0 0.1 eq.233
  227.1 0.1 eq.234
  227.2 0.1 lt.207
  227.2 0.1 lt.208
  227.3 0.1 reshape.450
  227.4 0.2 select_reduce_fusion.5
  227.6 0.1 reduce_sum.230
  227.7 0.1 reduce_sum.231
  227.8 0.1 reduce_sum.233
  227.9 0.1 reduce_sum.234
  228.0 0.0 copy-done
  228.0 0.5 multiply_multiply_fusion
  228.6 10.5 %copy.21 = bf16[1,32,8,128,128]{4,3,2,1,0:T(8,128)(2,1)} copy(bf16[1,32,8,128,128]{4,3,2,1,0:T(8,128)(2,1)} %get-tuple-element.715) | data formatting | bytes 16777216
  (22 shorter events, 0.2 us)
Async XLA Ops:
  11.3 216.7 %copy-start = (f32[7]{0:T(128)S(1)}, f32[7]{0:T(128)}, u32[]{:S(2)}) copy-start(f32[7]{0:T(128)} %constant.345.clone) | copy-start | bytes 88

commit v3 on v2

--- a/solution.py
+++ b/solution.py
@@ -14,7 +14,7 @@
 AXES = ("gx", "gy", "gz")
 MESH = pl.DeviceIdType.MESH
 LANES = 128
-SHARES = (2, 3, 4, 8)
+SHARES = (3, 4, 8)
 
 
 def bisect_cuts(histogram):
@@ -180,7 +180,10 @@
         return ((spot // count_z) * count_y + row) * count_z + spot % count_z
 
     def step_parts(step):
-        return step // count_y, step % count_y
+        later = (step // halves + count_y - 2) // (count_y - 1)
+        turn = step - halves + halves * (count_y - 1)
+        half = (1 - later) * step + later * (turn // (count_y - 1) - halves)
+        return half, later * (turn % (count_y - 1) + 1)
 
     def forward_copy(step, away):
         half, offset = step_parts(step)
@@ -218,8 +221,17 @@
         is_early = jnp.full(early.shape, place, jnp.int32) < first
         return jnp.where(is_early, early, late)
 
+    def step_of(half, offset):
+        return half if offset == 0 else halves + half * (count_y - 1) + offset - 1
+
+    def turn_of(half, offset):
+        step = step_of(half, offset)
+        if step < halves:
+            return 0
+        return step if step <= halves + count_y - 2 else step - 1
+
     def forward(half, offset):
-        step = half * count_y + offset
+        step = step_of(half, offset)
         if offset > 0:
             z_copy(half, offset).wait_recv()
 
@@ -278,14 +290,13 @@
 
             out_copy(step, away).start()
 
-    @pl.loop(0, steps + 1)
+    @pl.loop(0, steps)
     def _(step):
-        for half in range(halves):
-            for offset in range(count_y):
-
-                @pl.when(step == half * count_y + offset)
-                def _():
-                    forward(half, offset)
+        for half, offset in [(half, 0) for half in range(halves)] + pieces:
+
+            @pl.when(step == turn_of(half, offset))
+            def _():
+                forward(half, offset)
 
         @pl.when(step == 0)
         def _():
@@ -307,9 +318,7 @@
                 if stage < 2:
                     hist_start(stage + 1)
 
-        @pl.when(step > 0)
-        def _():
-            compute(step - 1)
+        compute(step)
 
     for piece in pieces:
         z_copy(*piece).wait_send()

time: 240 us -> 226 us (0.942)
  Pallas kernels: 208 us -> 195 us
    pallas_call x1, Pallas kernels: 208 us -> 195 us  [per_device(): lax.switch(choice, [relay(index, limit) for index, limit in enumerate(lim...]
where the time goes in v3:
time: 226 us
  Pallas kernels  195 us (86%)
  local copies, waits for them, and re-layouts  14.9 us (7%)
  other arithmetic  11.6 us (5%)
  between operations  4.1 us (2%)
    pallas_call x1, Pallas kernels, per_device(): lax.switch(choice, [relay(index, limit) for index, limit in enumerate(lim...  195 us
    unnamed x3, local copies, waits for them, and re-layouts  10.5 us

profile of v3, /device:TPU:25, one launch (start us, length us, event | category | flops | bytes accessed | tf_op | source)
XLA Modules:
  0.0 225.7 jit_solution(10981372318093399882)
XLA Ops:
  0.6 0.0 copy-start
  0.7 0.7 slice_bitcast_fusion
  1.4 0.1 broadcast_select_fusion
  1.5 0.1 broadcast_select_fusion.1
  1.6 0.7 and_select_fusion.2
  2.3 0.1 convert_reduce_fusion.1
  2.5 0.1 and_convert_fusion
  2.6 0.7 constant_dynamic-slice_fusion.3
  3.3 0.1 convert_reduce_fusion.3
  3.4 0.1 iota_compare_fusion.1
  3.5 0.1 convert_reduce_fusion
  3.7 0.1 minimum_reduce_fusion
  3.8 0.7 compare_convert_fusion
  5.2 0.9 convert_reduce_fusion.4
  6.2 0.6 reduce_max.23
  6.8 0.6 reduce_max.24
  8.8 0.6 reduce_max.29
  10.1 0.6 reduce_max.38
  11.3 199.3 %conditional.1 = (s32[56,128]{1,0:T(8,128)S(1)}, bf16[1,32,8,128,128]{4,3,2,1,0:T(8,128)(2,1)}) conditional(s32[]{:T(128)} %clamp.11, (s32[1,128]{1,0:T(1,128)S(1)}, s32[1,128]{1,0:T(1,128)S(1)}, s32[1,128]{1,0:T(1,128)S(1)}, s32[1,128]{1,0:T(1,128)S(1)}, s32[1,128]{1,0:T(1,128)S(1)}, /*index=5*/s32[128,128]{1,0:T(8,128)S(1)}, ...), branch_computations={%region_12.16_spmd, %region_16.20_spmd, %region_20.24_spmd} | conditional | flops 136038 | bytes 481112 | solution.py:490
  11.4 1.4 fusion.export_ref
  12.8 0.6 reshape.412.forward_ref
  13.4 0.6 reshape.413.cost_ref
  14.0 0.1 reduce_sum.143
  14.1 0.1 compare_select_fusion
  14.2 0.7 select_n.278.gain_ref
  14.9 0.7 select_reduce_fusion.pack_ref
  15.5 195.1 %relay_forces_44.2 = (bf16[32,8,128,128]{3,2,1,0:T(8,128)(2,1)}, s32[56,128]{1,0:T(8,128)S(1)}) custom-call(s32[256]{0:T(256)} %select_reduce_fusion.pack_ref, s32[256]{0:T(256)} %reshape.412.forward_ref, f32[256]{0:T(256)} %select_n.278.gain_ref, bf16[128,128,128]{2,1,0:T(8,128)(2,1)} %get-tuple-element.509.rows_ref, bf16[128,128]{1,0:T(8,128)(2,1)} %fusion.export_ref, ...), custom_call_target="tpu_custom_call" | custom-call | tf_op jit(solution)/shard_map/cond/branch_0_fun/relay_forces_44/pallas_call | solution.py:490
  210.6 2.0 reduce-window.6
  212.6 0.3 slice_reduce_fusion
  212.9 0.2 reduce-window.9
  213.1 0.1 broadcast_add_fusion
  213.1 0.2 copy.10
  213.4 0.3 convert_reduce_fusion.2
  213.7 0.1 eq.215
  213.8 0.1 eq.216
  213.8 0.1 lt.196
  213.9 0.1 lt.197
  214.0 0.1 reshape.425
  214.1 0.2 select_reduce_fusion.4
  214.3 0.1 reduce_sum.207
  214.4 0.1 reduce_sum.208
  214.5 0.1 reduce_sum.210
  214.6 0.1 reduce_sum.211
  214.7 0.0 copy-done
  214.7 0.5 multiply_multiply_fusion
  215.2 10.5 %copy.19 = bf16[1,32,8,128,128]{4,3,2,1,0:T(8,128)(2,1)} copy(bf16[1,32,8,128,128]{4,3,2,1,0:T(8,128)(2,1)} %get-tuple-element.543) | data formatting | bytes 16777216
  (22 shorter events, 0.2 us)
Async XLA Ops:
  0.6 214.1 %copy-start = (f32[7]{0:T(128)S(1)}, f32[7]{0:T(128)}, u32[]{:S(2)}) copy-start(f32[7]{0:T(128)} %constant.318.clone) | copy-start | bytes 88
